TPU v7x, 32 devices: a whole 2x2x4 slice. The times are simulated.
32 devices in a mesh: seg: 8 (over y, x, core), col: 4 (over z).
Axes of the slice: x: 2, y: 2, z: 4, core: 2. Of those that a mesh axis runs over, the one named last changes fastest.
Arguments:
- diagonal: float32 [32, 512, 512], P('seg', None, 'col'), as said below
- lower: float32 [32, 512, 512], P('seg'), as said below
- right_side: float32 [32, 512, 512], P('seg', None, 'col'), may hold values from -0.375 to 0.375
Outputs:
- solution: float32 [32, 512, 512], P('seg', None, 'col')
Inputs may be any that keep to these rules, and one draw needn't show every extreme that they name: Every diagonal block is symmetric, and with lower it makes A symmetric positive definite. `lower`: with diagonal it makes A symmetric positive definite.
All inputs are finite; a program needn't handle non-finite values.
Results may differ from a plain program's by a relative error of at most 0.0003.
Values sent between devices are 32-bit elements; how exact they have to be, the bound alone decides.
A program may use at most 192 MiB of HBM per device.

v0:
```python
import jax
import jax.numpy as jnp
from jax import lax
from jax.sharding import PartitionSpec as P


def passed_along(shard, axis, by):
    size = lax.axis_size(axis)
    pairs = [(i, i + by) for i in range(size) if 0 <= i + by < size]
    return lax.ppermute(shard, axis, pairs)


def matmul(left_hand, right_hand):
    return jnp.dot(
        left_hand, right_hand, precision=lax.Precision.HIGHEST, preferred_element_type=jnp.float32
    )


def invert_spd(matrix):
    factor = jnp.linalg.cholesky(matrix)
    identity = jnp.eye(matrix.shape[0], dtype=jnp.float32)
    inverse_factor = lax.linalg.triangular_solve(factor, identity, left_side=True, lower=True)
    return matmul(inverse_factor.T, inverse_factor)


def backward_sweep(inverses, next_links, advanced):

    def backward(later_block, inputs):
        inverse, advanced_block, coupling = inputs
        solved = matmul(inverse, advanced_block - matmul(coupling.T, later_block))
        return (solved, solved)

    last_state, solved = lax.scan(
        backward, jnp.zeros_like(advanced[0]), (inverses, advanced, next_links), reverse=True
    )
    return solved


def on_device(diagonal, lower, right_side):
    blocks = lower.shape[0]
    block_size = lower.shape[1]
    col_share = diagonal.shape[2]
    rhs_cols = right_side.shape[2]
    interior = blocks - 1
    offset = lax.axis_index("col") * col_share
    has_left = (lax.axis_index("seg") > 0).astype(jnp.float32)
    left_block = lower[0] * has_left
    sep_block = lower[blocks - 1]
    identity = jnp.eye(block_size, dtype=jnp.float32)
    left_mask = (jnp.arange(interior) > 0).astype(jnp.float32)[:, None, None]
    couple = lower[:interior] * left_mask
    next_links = jnp.concatenate(
        [couple[1:], jnp.zeros((1, block_size, block_size), jnp.float32)], axis=0
    )
    left_cols = lax.dynamic_slice_in_dim(left_block, offset, col_share, 1)
    right_cols = lax.dynamic_slice_in_dim(sep_block, offset, col_share, 0).T
    empty_cols = jnp.zeros((interior, block_size, col_share), jnp.float32)
    stacked = jnp.concatenate(
        [
            empty_cols.at[0].set(left_cols),
            empty_cols.at[interior - 1].set(right_cols),
            right_side[:interior],
        ],
        axis=2,
    )
    diag_items = lax.all_gather(diagonal[:interior], "col", axis=2, tiled=True)

    def forward(state, inputs):
        inverse, previous = state
        diag_block, coupling, rhs_block = inputs
        schur = diag_block - matmul(coupling, matmul(inverse, coupling.T))
        new_inverse = invert_spd(schur)
        advanced = rhs_block - matmul(coupling, matmul(inverse, previous))
        return ((new_inverse, advanced), (new_inverse, advanced))

    start_state = (identity, jnp.zeros((block_size, stacked.shape[2]), jnp.float32))
    final_state, (inverses, advanced) = lax.scan(
        forward, start_state, (diag_items, couple, stacked)
    )
    solved = backward_sweep(inverses, next_links, advanced)
    own_terms = matmul(sep_block, solved[interior - 1])
    next_terms = passed_along(matmul(left_block.T, solved[0]), "seg", -1)
    pivot_block = (
        diagonal[blocks - 1] - own_terms[:, col_share : 2 * col_share] - next_terms[:, :col_share]
    )
    sub_block = -own_terms[:, :col_share]
    super_block = -next_terms[:, col_share : 2 * col_share]
    reduced_rhs = (
        right_side[blocks - 1] - own_terms[:, 2 * col_share :] - next_terms[:, 2 * col_share :]
    )
    levels = (lax.axis_size("seg") - 1).bit_length()
    for level_bit in range(levels):
        stride = 1 << level_bit
        pivot_full, sub_full, super_full = (
            lax.all_gather(pivot_block, "col", axis=1, tiled=True),
            lax.all_gather(sub_block, "col", axis=1, tiled=True),
            lax.all_gather(super_block, "col", axis=1, tiled=True),
        )
        pivot_inverse = invert_spd(pivot_full)
        scaled = matmul(
            pivot_inverse, jnp.concatenate([sub_block, super_block, reduced_rhs], axis=1)
        )
        lower_terms = passed_along(scaled, "seg", stride)
        upper_terms = passed_along(scaled, "seg", -stride)
        narrow = sub_block.shape[1]
        new_sub = -matmul(sub_full, lower_terms[:, :narrow])
        new_super = -matmul(super_full, upper_terms[:, narrow : 2 * narrow])
        pivot_block = (
            pivot_block
            - matmul(sub_full, lower_terms[:, narrow : 2 * narrow])
            - matmul(super_full, upper_terms[:, :narrow])
        )
        reduced_rhs = (
            reduced_rhs
            - matmul(sub_full, lower_terms[:, 2 * narrow :])
            - matmul(super_full, upper_terms[:, 2 * narrow :])
        )
        sub_block, super_block = (new_sub, new_super)
    pivot_full = lax.all_gather(pivot_block, "col", axis=1, tiled=True)
    separator = matmul(invert_spd(pivot_full), reduced_rhs)
    left_sep = passed_along(separator, "seg", 1)
    correction = jnp.zeros((interior, block_size, rhs_cols), jnp.float32)
    correction = correction.at[0].add(matmul(left_block, left_sep))
    correction = correction.at[interior - 1].add(matmul(sep_block.T, separator))
    previous_inverses = jnp.concatenate([identity[None], inverses[:-1]], axis=0)

    def forward_only(previous, inputs):
        inverse, coupling, rhs_block = inputs
        advanced_block = rhs_block - matmul(coupling, matmul(inverse, previous))
        return (advanced_block, advanced_block)

    last_pushed, pushed = lax.scan(
        forward_only,
        jnp.zeros((block_size, rhs_cols), jnp.float32),
        (previous_inverses, couple, correction),
    )
    adjust = backward_sweep(inverses, next_links, pushed)
    interior_part = solved[:, :, 2 * col_share :] - adjust
    return jnp.concatenate([interior_part, separator[None]], axis=0)


def solution(mesh):
    in_specs = (P("seg", None, "col"), P("seg", None, None), P("seg", None, "col"))
    out_specs = P("seg", None, "col")
    return jax.shard_map(
        on_device, mesh=mesh, in_specs=in_specs, out_specs=out_specs, check_vma=False
    )
```

profile of v0, /device:TPU:4, one launch (start us, length us, event | category | flops | bytes accessed | tf_op | source)
XLA Modules:
  0.0 1538.1 jit_solution(16074768213679367527)
XLA Ops:
  20.0 53.7 %all-gather.12.cloned.1.call-done = f32[3,512,512]{1,2,0:T(8,128)} async-done(((f32[3,512,128]{1,2,0:T(8,128)}), f32[3,512,512]{1,2,0:T(8,128)}) %all-gather.12.cloned.1.call-update) | async-done | bytes 3145744 | tf_op jit(solution)/shard_map/all_gather | solution.py:66
  75.2 486.3 %while.80 = (s32[]{:T(128)}, f32[512,512]{1,0:T(8,128)}, f32[512,384]{1,0:T(8,128)}, f32[3,512,512]{2,1,0:T(8,128)}, f32[3,512,384]{2,1,0:T(8,128)}, /*index=5*/...) while((s32[]{:T(128)}, f32[512,512]{1,0:T(8,128)}, ...), condition=%wide.region_9.12_spmd.clone, body=%wide.region_0.11_spmd.clone.sunk | while | flops 8661697536 | bytes 65018872 | solution.py:77
  83.5 11.7 cholesky.1691
  105.9 23.0 %cholesky.1694 = f32[128,128]{1,0:T(8,128)S(1)} custom-call(f32[128,128]{1,0:T(8,128)S(1)} %cholesky.1693), custom_call_target="Cholesky" | custom-call | tf_op jit(solution)/shard_map/while/body/eval_jaxpr/jit(cholesky)/cholesky | solution.py:20
  141.2 11.7 cholesky.1696
  164.6 11.7 cholesky.1697
  185.8 39.3 %custom-call.72 = f32[4,128,128]{1,2,0:T(8,128)S(1)} custom-call(f32[4,128,128]{2,1,0:T(8,128)S(1)} %get-tuple-element.966), custom_call_target="InvertDiagBlocksLowerTriangular" | custom-call | tf_op jit(solution)/shard_map/while/body/eval_jaxpr/triangular_solve/custom-call.3 | solution.py:22
  250.6 11.7 cholesky.1691
  273.0 12.1 cholesky.1694
  297.4 11.7 cholesky.1696
  320.9 11.7 cholesky.1697
  341.8 39.3 %custom-call.72 = f32[4,128,128]{1,2,0:T(8,128)S(1)} custom-call(f32[4,128,128]{2,1,0:T(8,128)S(1)} %get-tuple-element.966), custom_call_target="InvertDiagBlocksLowerTriangular" | custom-call | tf_op jit(solution)/shard_map/while/body/eval_jaxpr/triangular_solve/custom-call.3 | solution.py:22
  407.0 11.7 cholesky.1691
  429.4 11.9 cholesky.1694
  453.6 11.7 cholesky.1696
  477.0 11.7 cholesky.1697
  498.2 39.3 %custom-call.72 = f32[4,128,128]{1,2,0:T(8,128)S(1)} custom-call(f32[4,128,128]{2,1,0:T(8,128)S(1)} %get-tuple-element.966), custom_call_target="InvertDiagBlocksLowerTriangular" | custom-call | tf_op jit(solution)/shard_map/while/body/eval_jaxpr/triangular_solve/custom-call.3 | solution.py:22
  564.0 23.2 %while.77 = (s32[]{:T(128)}, f32[512,384]{1,0:T(8,128)}, f32[3,512,384]{2,1,0:T(8,128)}, f32[3,512,512]{2,1,0:T(8,128)}, f32[3,512,384]{2,1,0:T(8,128)}, /*index=5*/f32[3,512,512]{2,1,0:T(8,128)}, s32[]{:T(128)}, s32[]{:T(128)}) while((s32[]{:T(128)}, f32[512,384]{1,0:T(8,128)}, f32[3,512,384]{2,1,0:T(8,128)}, f32[3,512,512]{2,1,0:T(8,128)}, ...), condition=%wide.region_11.14_spmd, body=%wide.region_10.13_spmd.sunk | while | flops 2416115712 | bytes 6817889 | solution.py:33
  607.7 25.7 %all-gather.16.cloned.1.call-done = f32[512,512]{0,1:T(8,128)} async-done(((f32[512,128]{0,1:T(8,128)}), f32[512,512]{0,1:T(8,128)}) %all-gather.16.cloned.1.call-update) | async-done | bytes 1048592 | tf_op jit(solution)/shard_map/all_gather | solution.py:95
  638.7 11.7 cholesky.622
  664.6 11.7 cholesky.641
  689.3 11.7 cholesky.662
  714.4 11.7 cholesky.679
  733.5 11.9 while.82
  746.1 40.1 %custom-call.48 = f32[4,128,128]{1,2,0:T(8,128)S(1)} custom-call(f32[4,128,128]{2,1,0:T(8,128)} %copy-done.33), custom_call_target="InvertDiagBlocksLowerTriangular" | custom-call | tf_op jit(solution)/shard_map/triangular_solve/custom-call.3 | solution.py:22
  804.4 13.8 collective-permute-done.2
  835.8 16.7 %all-gather.22.cloned.1.call-done = f32[512,512]{0,1:T(8,128)} async-done(((f32[512,128]{0,1:T(8,128)}), f32[512,512]{0,1:T(8,128)}) %all-gather.22.cloned.1.call-update) | async-done | bytes 1048592 | tf_op jit(solution)/shard_map/all_gather | solution.py:95
  857.8 11.7 cholesky.694
  883.7 12.1 cholesky.713
  935.1 11.9 cholesky.751
  953.2 11.8 while.83
  965.7 40.1 %custom-call.52 = f32[4,128,128]{1,2,0:T(8,128)S(1)} custom-call(f32[4,128,128]{2,1,0:T(8,128)} %copy-done.34), custom_call_target="InvertDiagBlocksLowerTriangular" | custom-call | tf_op jit(solution)/shard_map/triangular_solve/custom-call.3 | solution.py:22
  1026.4 14.9 collective-permute-done.4
  1043.5 14.2 collective-permute-done.3
  1071.6 17.2 %all-gather.28.cloned.1.call-done = f32[512,512]{0,1:T(8,128)} async-done(((f32[512,128]{0,1:T(8,128)}), f32[512,512]{0,1:T(8,128)}) %all-gather.28.cloned.1.call-update) | async-done | bytes 1048592 | tf_op jit(solution)/shard_map/all_gather | solution.py:95
  1119.9 11.9 cholesky.785
  1171.2 11.9 cholesky.823
  1189.4 11.8 while.84
  1201.9 40.1 %custom-call.56 = f32[4,128,128]{1,2,0:T(8,128)S(1)} custom-call(f32[4,128,128]{2,1,0:T(8,128)} %copy-done.35), custom_call_target="InvertDiagBlocksLowerTriangular" | custom-call | tf_op jit(solution)/shard_map/triangular_solve/custom-call.3 | solution.py:22
  1260.7 14.0 collective-permute-done.6
  1287.5 23.1 %all-gather.32.cloned.1.call-done = f32[512,512]{0,1:T(8,128)} async-done(((f32[512,128]{0,1:T(8,128)}), f32[512,512]{0,1:T(8,128)}) %all-gather.32.cloned.1.call-update) | async-done | bytes 1048592 | tf_op jit(solution)/shard_map/all_gather | solution.py:119
  1342.5 11.9 cholesky.857
  1370.1 13.2 cholesky.878
  1399.7 11.9 cholesky.895
  1418.5 14.2 while.85
  1432.7 40.7 %custom-call.60 = f32[4,128,128]{1,2,0:T(8,128)} custom-call(f32[4,128,128]{2,1,0:T(8,128)} %get-tuple-element.463), custom_call_target="InvertDiagBlocksLowerTriangular" | custom-call | tf_op jit(solution)/shard_map/triangular_solve/custom-call.3 | solution.py:22
  1498.4 14.6 while.81
  1513.1 16.0 %while.78 = (s32[]{:T(128)}, f32[512,128]{1,0:T(8,128)S(1)}, f32[3,512,128]{2,1,0:T(8,128)S(1)}, f32[3,512,512]{2,1,0:T(8,128)}, f32[3,512,128]{2,1,0:T(8,128)},...) while((s32[]{:T(128)}, f32[512,128]{1,0:T(8,128)S(1)}, f32[3,512,128]{2,1,0:T(8,128)S(1)}, ...), condition=%wide.region_15.18_spmd, body=%wide.region_14.17_spmd.sunk | while | flops 805371904 | bytes 3672161 | solution.py:33
  (551 shorter events, 751.7 us)
Async XLA Ops:
  6.5 67.2 %all-gather.12.cloned.1.call-start = ((), (), s32[]{:S(2)}) async-start(), calls=%async_computation | async-start | bytes 3932160 | tf_op jit(solution)/shard_map/all_gather | solution.py:66
  8.9 624.5 %all-gather.16.cloned.1.call-start = ((), (), s32[]{:S(2)}) async-start(), calls=%async_computation.2 | async-start | bytes 1310720 | tf_op jit(solution)/shard_map/all_gather | solution.py:95
  11.9 3.0 copy-start.6
  15.5 3.0 slice-start
  75.6 3.9 copy-start
  228.7 9.7 copy-start.1
  242.7 3.9 copy-start
  384.7 9.9 copy-start.1
  399.1 3.9 copy-start
  541.1 10.0 copy-start.1
  587.2 10.0 slice-start.1
  591.1 12.4 collective-permute-start
  605.9 198.5 %all-gather.18.cloned.1.call-start = ((), (), s32[]{:S(2)}) async-start(), calls=%async_computation.3 | async-start | bytes 1310720 | tf_op jit(solution)/shard_map/all_gather | solution.py:97
  606.7 213.6 %all-gather.14.cloned.1.call-start = ((), (), s32[]{:S(2)}) async-start(), calls=%async_computation.1 | async-start | bytes 1310720 | tf_op jit(solution)/shard_map/all_gather | solution.py:96
  607.2 245.2 %all-gather.22.cloned.1.call-start = ((), (), s32[]{:S(2)}) async-start(), calls=%async_computation.5 | async-start | bytes 1310720 | tf_op jit(solution)/shard_map/all_gather | solution.py:95
  786.3 2.9 copy-start.30
  789.6 7.7 copy-start.14
  789.6 7.7 copy-start.15
  789.6 7.7 copy-start.20
  800.0 18.1 %collective-permute-start.2 = (f32[512,384]{1,0:T(8,128)}, f32[512,384]{1,0:T(8,128)}, u32[]{:S(2)}, u32[]{:S(2)}) collective-permute-start(f32[512,384]{1,0:T(8,128)} %fusion.137), channel_id=1, source_target_pairs={{4,0},{8,4},{12,8},{16,12},{20,16},{24,20},{28,24},{5,1},{9,5},{13... | collective-permute-start | bytes 2359304 | tf_op jit(solution)/shard_map/ppermute | solution.py:10
  802.4 19.7 %collective-permute-start.1 = (f32[512,384]{1,0:T(8,128)}, f32[512,384]{1,0:T(8,128)}, u32[]{:S(2)}, u32[]{:S(2)}) collective-permute-start(f32[512,384]{1,0:T(8,128)} %fusion.137), channel_id=1, source_target_pairs={{0,4},{4,8},{8,12},{12,16},{16,20},{20,24},{24,28},{1,5},{5,9},{9,... | collective-permute-start | bytes 2359304 | tf_op jit(solution)/shard_map/ppermute | solution.py:10
  824.9 8.0 copy-start.21
  825.0 201.5 %all-gather.24.cloned.1.call-start = ((), (), s32[]{:S(2)}) async-start(), calls=%async_computation.6 | async-start | bytes 1310720 | tf_op jit(solution)/shard_map/all_gather | solution.py:97
  827.8 215.6 %all-gather.20.cloned.1.call-start = ((), (), s32[]{:S(2)}) async-start(), calls=%async_computation.4 | async-start | bytes 1310720 | tf_op jit(solution)/shard_map/all_gather | solution.py:96
  830.6 258.1 %all-gather.28.cloned.1.call-start = ((), (), s32[]{:S(2)}) async-start(), calls=%async_computation.8 | async-start | bytes 1310720 | tf_op jit(solution)/shard_map/all_gather | solution.py:95
  1005.9 2.9 copy-start.31
  1009.2 7.7 copy-start.16
  1009.2 7.7 copy-start.18
  1009.2 7.7 copy-start.22
  1019.7 21.7 %collective-permute-start.4 = (f32[512,384]{1,0:T(8,128)}, f32[512,384]{1,0:T(8,128)}, u32[]{:S(2)}, u32[]{:S(2)}) collective-permute-start(f32[512,384]{1,0:T(8,128)} %fusion.148), channel_id=1, source_target_pairs={{8,0},{12,4},{16,8},{20,12},{24,16},{28,20},{9,1},{13,5},{17,9},{2... | collective-permute-start | bytes 2359304 | tf_op jit(solution)/shard_map/ppermute | solution.py:10
  1023.2 34.5 %collective-permute-start.3 = (f32[512,384]{1,0:T(8,128)}, f32[512,384]{1,0:T(8,128)}, u32[]{:S(2)}, u32[]{:S(2)}) collective-permute-start(f32[512,384]{1,0:T(8,128)} %fusion.148), channel_id=1, source_target_pairs={{0,8},{4,12},{8,16},{12,20},{16,24},{20,28},{1,9},{5,13},{9,17},{1... | collective-permute-start | bytes 2359304 | tf_op jit(solution)/shard_map/ppermute | solution.py:10
  1060.5 8.3 copy-start.23
  1060.5 200.2 %all-gather.30.cloned.1.call-start = ((), (), s32[]{:S(2)}) async-start(), calls=%async_computation.9 | async-start | bytes 1310720 | tf_op jit(solution)/shard_map/all_gather | solution.py:97
  1063.4 213.4 %all-gather.26.cloned.1.call-start = ((), (), s32[]{:S(2)}) async-start(), calls=%async_computation.7 | async-start | bytes 1310720 | tf_op jit(solution)/shard_map/all_gather | solution.py:96
  1066.2 244.4 %all-gather.32.cloned.1.call-start = ((), (), s32[]{:S(2)}) async-start(), calls=%async_computation.10 | async-start | bytes 1310720 | tf_op jit(solution)/shard_map/all_gather | solution.py:119
  1242.0 2.9 copy-start.32
  1245.3 7.7 copy-start.17
  1245.3 7.7 copy-start.19
  1245.3 7.7 copy-start.24
  1255.8 18.9 %collective-permute-start.6 = (f32[512,384]{1,0:T(8,128)}, f32[512,384]{1,0:T(8,128)}, u32[]{:S(2)}, u32[]{:S(2)}) collective-permute-start(f32[512,384]{1,0:T(8,128)} %fusion.159), channel_id=1, source_target_pairs={{16,0},{20,4},{24,8},{28,12},{17,1},{21,5},{25,9},{29,13},{18,2},{... | collective-permute-start | bytes 2359304 | tf_op jit(solution)/shard_map/ppermute | solution.py:10
  1259.0 20.7 %collective-permute-start.5 = (f32[512,384]{1,0:T(8,128)}, f32[512,384]{1,0:T(8,128)}, u32[]{:S(2)}, u32[]{:S(2)}) collective-permute-start(f32[512,384]{1,0:T(8,128)} %fusion.159), channel_id=1, source_target_pairs={{0,16},{4,20},{8,24},{12,28},{1,17},{5,21},{9,25},{13,29},{2,18},{... | collective-permute-start | bytes 2359304 | tf_op jit(solution)/shard_map/ppermute | solution.py:10
  1473.4 5.6 copy-start.29
  1477.5 6.0 copy-start.27
  1481.1 5.7 copy-start.4
  1484.5 9.7 copy-start.25
  1484.5 8.6 collective-permute-start.7
  1487.0 6.1 copy-start.7
  1513.0 17.2 %copy-start.26 = (f32[512,128]{1,0:T(8,128)S(1)}, f32[512,128]{1,0:T(8,128)}, u32[]{:S(2)}) copy-start(f32[512,128]{1,0:T(8,128)} %copy-done.25) | copy-start | bytes 786436
  (19 other events, 20.7 us)
Sparse Core Ops, SparseCore 0:
  9.0 64.6 all-gather.11
  606.0 27.3 all-gather.15
  635.0 27.3 all-gather.17
  663.8 27.3 all-gather.13
  825.1 27.3 all-gather.21
  853.9 27.5 all-gather.23
  883.0 27.4 all-gather.19
  1060.6 28.0 all-gather.27
  1090.3 27.2 all-gather.29
  1119.0 27.5 all-gather.25
  1282.7 27.8 all-gather.31
where the time goes:
time: 1540 us
  other arithmetic  884 us (57%)
  matrix products  268 us (17%)
  waiting for transfers between devices  205 us (13%)
  local copies, waits for them, and re-layouts  116 us (8%)
  between operations  24.9 us (2%)
  starting transfers between devices  22.1 us (1%)
  loops' own time  17.1 us (1%)
    another operation x101, other arithmetic, invert_spd(): factor = jnp.linalg.cholesky(matrix)  575 us
    another operation x21, other arithmetic, invert_spd(): lax.linalg.triangular_solve(factor, identity, left_side=True, lower=True)  289 us
    dot_general x61, matrix products, matmul(): jnp.dot(left_hand, right_hand, precision=lax.Precision.HIGHEST, preferred...  180 us
    another operation x92, local copies, waits for them, and re-layouts, invert_spd(): lax.linalg.triangular_solve(factor, identity, left_side=True, lower=True)  72.6 us
    ppermute x8, waiting for transfers between devices, passed_along(): return lax.ppermute(shard, axis, pairs)  67.1 us
    all_gather x3, waiting for transfers between devices, on_device(): lax.all_gather(pivot_block, 'col', axis=1, tiled=True)  59.6 us
    all_gather x1, waiting for transfers between devices, on_device(): diag_items = lax.all_gather(diagonal[:interior], 'col', axis=2, tiled=True)  53.7 us
    another operation x49, matrix products, invert_spd(): lax.linalg.triangular_solve(factor, identity, left_side=True, lower=True)  49.3 us
  transfers between devices with their start and end apart: 19, of which 13 were waited for; matrix products, arithmetic and copies ran while one was open for 35% of the time, Pallas kernels for 0%

commit v1 on v0

--- a/solution.py
+++ b/solution.py
@@ -1,6 +1,8 @@
 import jax
 import jax.numpy as jnp
 from jax import lax
+from jax.experimental import pallas as pl
+from jax.experimental.pallas import tpu as pltpu
 from jax.sharding import PartitionSpec as P
 
 
@@ -16,11 +18,99 @@
     )
 
 
+TILE = 128
+SUB = 8
+
+
+def lanes_of(tile, lane):
+    return jnp.broadcast_to(tile[:, lane : lane + 1], tile.shape)
+
+
+def rows_of(tile, row):
+    return jnp.broadcast_to(tile[row : row + 1, :], tile.shape)
+
+
+def invert_tile(rows):
+    lane = lax.broadcasted_iota(jnp.int32, (SUB, TILE), 1)
+    sublane = lax.broadcasted_iota(jnp.int32, (SUB, TILE), 0)
+    rows = list(rows)
+    for panel in range(TILE // SUB):
+        first = panel * SUB
+        inside = (lane >= first) & (lane < first + SUB)
+        own = rows[panel]
+        inverse = [lanes_of(own, first + i) for i in range(SUB)]
+        for r in range(SUB):
+            at_r = sublane == r
+            scale = 1.0 / rows_of(inverse[r], r)
+            pivot = jnp.where(at_r, 1.0, inverse[r]) * scale
+            for i in range(SUB):
+                if i != r:
+                    factor = rows_of(inverse[i], r)
+                    inverse[i] = jnp.where(at_r, 0.0, inverse[i]) - factor * pivot
+            inverse[r] = pivot
+        marked = jnp.where(inside, (lane - first == sublane).astype(jnp.float32), own)
+        swept = inverse[0] * rows_of(marked, 0)
+        for i in range(1, SUB):
+            swept = swept + inverse[i] * rows_of(marked, i)
+        spread = [rows_of(swept, i) for i in range(SUB)]
+        for t in range(TILE // SUB):
+            if t != panel:
+                total = jnp.where(inside, 0.0, rows[t])
+                for i in range(SUB):
+                    total = total - lanes_of(rows[t], first + i) * spread[i]
+                rows[t] = total
+        rows[panel] = swept
+    return jnp.concatenate(rows, axis=0)
+
+
+def invert_kernel(matrix_ref, out_ref):
+    count, size = matrix_ref.shape[0], matrix_ref.shape[1]
+    out_ref[...] = matrix_ref[...]
+    eye = (
+        lax.broadcasted_iota(jnp.int32, (TILE, TILE), 0)
+        == lax.broadcasted_iota(jnp.int32, (TILE, TILE), 1)
+    ).astype(jnp.float32)
+
+    def step(k, carry):
+        first = pl.multiple_of(k * TILE, TILE)
+        here = pl.ds(first, TILE)
+        tiles = []
+        for m in range(count):
+            rows = [
+                out_ref[m, pl.ds(pl.multiple_of(first + t * SUB, SUB), SUB), here]
+                for t in range(TILE // SUB)
+            ]
+            tiles.append(invert_tile(rows))
+        for m in range(count):
+            out_ref[m, here, here] = jnp.zeros((TILE, TILE), jnp.float32)
+            column = out_ref[m, :, here]
+            out_ref[m, :, here] = jnp.zeros((size, TILE), jnp.float32)
+            out_ref[m, here, here] = eye
+            swept = matmul(tiles[m], out_ref[m, here, :])
+            out_ref[m] = out_ref[m] - matmul(column, swept)
+            out_ref[m, here, :] = swept
+        return carry
+
+    lax.fori_loop(0, size // TILE, step, 0)
+
+
+def invert_batch(matrices):
+    count, size = matrices.shape[0], matrices.shape[1]
+    return pl.pallas_call(
+        invert_kernel,
+        out_shape=jax.ShapeDtypeStruct(matrices.shape, jnp.float32),
+        in_specs=[pl.BlockSpec(memory_space=pltpu.VMEM)],
+        out_specs=pl.BlockSpec(memory_space=pltpu.VMEM),
+        cost_estimate=pl.CostEstimate(
+            flops=2 * count * size**3, bytes_accessed=8 * count * size**2, transcendentals=0
+        ),
+        compiler_params=pltpu.CompilerParams(vmem_limit_bytes=32 * 2**20),
+        name="invert_spd",
+    )(matrices)
+
+
 def invert_spd(matrix):
-    factor = jnp.linalg.cholesky(matrix)
-    identity = jnp.eye(matrix.shape[0], dtype=jnp.float32)
-    inverse_factor = lax.linalg.triangular_solve(factor, identity, left_side=True, lower=True)
-    return matmul(inverse_factor.T, inverse_factor)
+    return invert_batch(matrix[None])[0]
 
 
 def backward_sweep(inverses, next_links, advanced):

time: 1540 us -> 643 us (0.42)
  other arithmetic: 884 us -> 14.2 us
  Pallas kernels: 0 us -> 173 us
  matrix products: 268 us -> 163 us
  local copies, waits for them, and re-layouts: 116 us -> 20.9 us
  loops' own time: 17.1 us -> 0.34 us
  waiting for transfers between devices: 205 us -> 221 us
    another operation x122 -> x0, other arithmetic: 865 us -> none  [the longest x101 575 us: invert_spd(): factor = jnp.linalg.cholesky(matrix)]
    pallas_call x0 -> x7, Pallas kernels: none -> 173 us  [invert_batch(): pl.pallas_call(invert_kernel, out_shape=jax.ShapeDtypeStruct(matrices.sha...]
    another operation x91 -> x0, matrix products: 87.8 us -> none  [the longest x49 49.3 us: invert_spd(): lax.linalg.triangular_solve(factor, identity, left_side=True, lower=True)]
    another operation x126 -> x6, local copies, waits for them, and re-layouts: 83.2 us -> 6.01 us  [the longest x92 72.6 us: invert_spd(): lax.linalg.triangular_solve(factor, identity, left_side=True, lower=True)]
    all_gather x3, waiting for transfers between devices: 0.06 us -> 21.9 us  [on_device(): lax.all_gather(sub_block, 'col', axis=1, tiled=True)]
    dot_general x61 -> x54, matrix products: 180 us -> 163 us  [matmul(): jnp.dot(left_hand, right_hand, precision=lax.Precision.HIGHEST, preferred...]
  transfers between devices with their start and end apart: 19 -> 19, of which waited for: 13 -> 14; matrix products, arithmetic and copies ran while one was open for 35% -> 10% of each run, Pallas kernels for 0% -> 12%
where the time goes in v1:
time: 643 us; the launch traced here: 631 us
  waiting for transfers between devices  221 us (34%)
  Pallas kernels  173 us (27%)
  matrix products  163 us (25%)
  starting transfers between devices  23.1 us (4%)
  local copies, waits for them, and re-layouts  20.9 us (3%)
  other arithmetic  14.2 us (2%)
  between operations  14.1 us (2%)
    pallas_call x7, Pallas kernels, invert_batch(): pl.pallas_call(invert_kernel, out_shape=jax.ShapeDtypeStruct(matrices.sha...  173 us
    dot_general x54, matrix products, matmul(): jnp.dot(left_hand, right_hand, precision=lax.Precision.HIGHEST, preferred...  163 us
    ppermute x8, waiting for transfers between devices, passed_along(): return lax.ppermute(shard, axis, pairs)  61 us
    all_gather x3, waiting for transfers between devices, on_device(): lax.all_gather(pivot_block, 'col', axis=1, tiled=True)  59.7 us
    all_gather x1, waiting for transfers between devices, on_device(): diag_items = lax.all_gather(diagonal[:interior], 'col', axis=2, tiled=True)  54.2 us
    all_gather x1, waiting for transfers between devices, on_device(): pivot_full = lax.all_gather(pivot_block, 'col', axis=1, tiled=True)  23.1 us
    ppermute x8, starting transfers between devices, passed_along(): return lax.ppermute(shard, axis, pairs)  22.1 us
    all_gather x3, waiting for transfers between devices, on_device(): lax.all_gather(sub_block, 'col', axis=1, tiled=True)  21.9 us
  transfers between devices with their start and end apart: 19, of which 14 were waited for; matrix products, arithmetic and copies ran while one was open for 10% of the time, Pallas kernels for 12%

profile of v1, /device:TPU:4, one launch (start us, length us, event | category | flops | bytes accessed | tf_op | source)
XLA Modules:
  0.0 630.7 jit_solution(11432730446459338970)
XLA Ops:
  19.4 54.2 %all-gather.12.cloned.1.call-done = f32[3,512,512]{2,1,0:T(8,128)} async-done(((f32[3,512,128]{2,1,0:T(8,128)}), f32[3,512,512]{2,1,0:T(8,128)}) %all-gather.12.cloned.1.call-update) | async-done | bytes 3145744 | tf_op jit(solution)/shard_map/all_gather | solution.py:156
  75.1 118.1 %while.68 = (s32[]{:T(128)}, f32[512,512]{1,0:T(8,128)S(1)}, f32[512,384]{1,0:T(8,128)}, f32[3,512,512]{2,1,0:T(8,128)}, f32[3,512,384]{2,1,0:T(8,128)}, /*index...) while((s32[]{:T(128)}, f32[512,512]{1,0:T(8,128)S(1)}, ...), condition=%wide.region_1.0_spmd.clone, body=%wide.region_0.0_spmd.clone.sunk | while | flops 5906235392 | bytes 18353264 | solution.py:167
  75.1 3.1 fusion.173
  78.2 3.4 fusion.174.matrix_ref
  83.4 24.7 %invert_spd.9 = f32[1,512,512]{2,1,0:T(8,128)S(1)} custom-call(f32[1,512,512]{2,1,0:T(8,128)S(1)} %fusion.174.matrix_ref), custom_call_target="tpu_custom_call" | custom-call | flops 268435456 | bytes 2097152 | tf_op jit(solution)/shard_map/while/body/eval_jaxpr/invert_spd/pallas_call | solution.py:99
  109.2 4.4 bitcast_dynamic-update-slice_fusion.10
  116.7 3.4 fusion.174.matrix_ref
  123.1 24.7 %invert_spd.9 = f32[1,512,512]{2,1,0:T(8,128)S(1)} custom-call(f32[1,512,512]{2,1,0:T(8,128)S(1)} %fusion.174.matrix_ref), custom_call_target="tpu_custom_call" | custom-call | flops 268435456 | bytes 2097152 | tf_op jit(solution)/shard_map/while/body/eval_jaxpr/invert_spd/pallas_call | solution.py:99
  148.9 4.4 bitcast_dynamic-update-slice_fusion.10
  153.3 3.1 fusion.173
  156.4 3.4 fusion.174.matrix_ref
  162.8 24.7 %invert_spd.9 = f32[1,512,512]{2,1,0:T(8,128)S(1)} custom-call(f32[1,512,512]{2,1,0:T(8,128)S(1)} %fusion.174.matrix_ref), custom_call_target="tpu_custom_call" | custom-call | flops 268435456 | bytes 2097152 | tf_op jit(solution)/shard_map/while/body/eval_jaxpr/invert_spd/pallas_call | solution.py:99
  188.6 4.4 bitcast_dynamic-update-slice_fusion.10
  196.2 22.3 %while.66 = (s32[]{:T(128)}, f32[512,384]{1,0:T(8,128)}, f32[3,512,384]{2,1,0:T(8,128)}, f32[3,512,512]{2,1,0:T(8,128)}, f32[3,512,384]{2,1,0:T(8,128)}, /*index=5*/f32[3,512,512]{2,1,0:T(8,128)S(1)}, s32[]{:T(128)}, s32[]{:T(128)}) while((s32[]{:T(128)}, f32[512,384]{1,0:T(8,128)}, f32[3,512,384]{2,1,0:T(8,128)}, f32[3,512,512]{2,1,0:T(8,128)}, ...), condition=%wide.region_3.4_spmd, body=%wide.region_2.3_spmd.sunk | while | flops 2416115712 | bytes 6817889 | solution.py:123
  196.2 3.2 convolution_subtract_fusion.13
  199.4 4.2 bitcast_dynamic-update-slice_fusion.8
  203.7 3.2 convolution_subtract_fusion.13
  206.9 4.2 bitcast_dynamic-update-slice_fusion.8
  211.1 3.2 convolution_subtract_fusion.13
  214.3 4.2 bitcast_dynamic-update-slice_fusion.8
  218.5 3.4 fusion.61
  224.7 3.3 convolution_bitcast_fusion
  228.1 6.2 collective-permute-done
  237.5 26.6 %all-gather.16.cloned.1.call-done = f32[512,512]{1,0:T(8,128)} async-done(((f32[512,128]{1,0:T(8,128)}), f32[512,512]{1,0:T(8,128)}) %all-gather.16.cloned.1.call-update) | async-done | bytes 1048592 | tf_op jit(solution)/shard_map/all_gather | solution.py:185
  265.3 24.9 %invert_spd.5 = f32[1,512,512]{2,1,0:T(8,128)S(1)} custom-call(f32[1,512,512]{2,1,0:T(8,128)S(1)} %bitcast.190), custom_call_target="tpu_custom_call" | custom-call | flops 268435456 | bytes 2097152 | tf_op jit(solution)/shard_map/invert_spd/pallas_call | solution.py:99
  290.3 3.8 fusion.56
  298.8 14.4 %collective-permute-done.2 = f32[512,384]{1,0:T(8,128)} collective-permute-done((f32[512,384]{1,0:T(8,128)}, f32[512,384]{1,0:T(8,128)}, u32[]{:S(2)}, u32[]{:S(2)}) %collective-permute-start.2) | collective-permute-done | bytes 786464 | tf_op jit(solution)/shard_map/ppermute | solution.py:12
  316.1 7.4 %all-gather.14.cloned.1.call-done = f32[512,512]{1,0:T(8,128)} async-done(((f32[512,128]{1,0:T(8,128)}), f32[512,512]{1,0:T(8,128)}) %all-gather.14.cloned.1.call-update) | async-done | bytes 1048592 | tf_op jit(solution)/shard_map/all_gather | solution.py:186
  323.6 3.1 fusion.49
  338.5 16.6 %all-gather.22.cloned.1.call-done = f32[512,512]{1,0:T(8,128)} async-done(((f32[512,128]{1,0:T(8,128)}), f32[512,512]{1,0:T(8,128)}) %all-gather.22.cloned.1.call-update) | async-done | bytes 1048592 | tf_op jit(solution)/shard_map/all_gather | solution.py:185
  356.3 24.7 %invert_spd.6 = f32[1,512,512]{2,1,0:T(8,128)S(1)} custom-call(f32[1,512,512]{2,1,0:T(8,128)S(1)} %bitcast.188), custom_call_target="tpu_custom_call" | custom-call | flops 268435456 | bytes 2097152 | tf_op jit(solution)/shard_map/invert_spd/pallas_call | solution.py:99
  381.0 3.7 fusion.54
  384.8 3.4 collective-permute-start.4
  388.1 3.4 collective-permute-start.3
  391.5 14.8 %collective-permute-done.4 = f32[512,384]{1,0:T(8,128)} collective-permute-done((f32[512,384]{1,0:T(8,128)}, f32[512,384]{1,0:T(8,128)}, u32[]{:S(2)}, u32[]{:S(2)}) %collective-permute-start.4) | collective-permute-done | bytes 786464 | tf_op jit(solution)/shard_map/ppermute | solution.py:12
  408.6 6.0 all-gather.20.cloned.1.call-done
  414.6 8.2 %collective-permute-done.3 = f32[512,384]{1,0:T(8,128)} collective-permute-done((f32[512,384]{1,0:T(8,128)}, f32[512,384]{1,0:T(8,128)}, u32[]{:S(2)}, u32[]{:S(2)}) %collective-permute-start.3) | collective-permute-done | bytes 786464 | tf_op jit(solution)/shard_map/ppermute | solution.py:12
  437.5 16.6 %all-gather.28.cloned.1.call-done = f32[512,512]{1,0:T(8,128)} async-done(((f32[512,128]{1,0:T(8,128)}), f32[512,512]{1,0:T(8,128)}) %all-gather.28.cloned.1.call-update) | async-done | bytes 1048592 | tf_op jit(solution)/shard_map/all_gather | solution.py:185
  455.4 24.7 %invert_spd.7 = f32[1,512,512]{2,1,0:T(8,128)S(1)} custom-call(f32[1,512,512]{2,1,0:T(8,128)S(1)} %bitcast.189), custom_call_target="tpu_custom_call" | custom-call | flops 268435456 | bytes 2097152 | tf_op jit(solution)/shard_map/invert_spd/pallas_call | solution.py:99
  480.1 3.7 fusion.52
  483.8 4.2 collective-permute-start.6
  489.5 13.3 %collective-permute-done.6 = f32[512,384]{1,0:T(8,128)} collective-permute-done((f32[512,384]{1,0:T(8,128)}, f32[512,384]{1,0:T(8,128)}, u32[]{:S(2)}, u32[]{:S(2)}) %collective-permute-start.6) | collective-permute-done | bytes 786464 | tf_op jit(solution)/shard_map/ppermute | solution.py:12
  505.1 8.5 %all-gather.26.cloned.1.call-done = f32[512,512]{1,0:T(8,128)} async-done(((f32[512,128]{1,0:T(8,128)}), f32[512,512]{1,0:T(8,128)}) %all-gather.26.cloned.1.call-update) | async-done | bytes 1048592 | tf_op jit(solution)/shard_map/all_gather | solution.py:186
  521.9 23.1 %all-gather.32.cloned.1.call-done = f32[512,512]{1,0:T(8,128)} async-done(((f32[512,128]{1,0:T(8,128)}), f32[512,512]{1,0:T(8,128)}) %all-gather.32.cloned.1.call-update) | async-done | bytes 1048592 | tf_op jit(solution)/shard_map/all_gather | solution.py:209
  546.2 24.7 %invert_spd.8 = f32[1,512,512]{2,1,0:T(8,128)S(1)} custom-call(f32[1,512,512]{2,1,0:T(8,128)S(1)} %bitcast.191), custom_call_target="tpu_custom_call" | custom-call | flops 268435456 | bytes 2097152 | tf_op jit(solution)/shard_map/invert_spd/pallas_call | solution.py:99
  577.3 4.1 collective-permute-done.7
  586.7 15.5 %while.69 = (s32[]{:T(128)}, f32[512,128]{1,0:T(8,128)S(1)}, f32[3,512,128]{2,1,0:T(8,128)}, f32[3,512,128]{2,1,0:T(8,128)}, f32[3,512,512]{2,1,0:T(8,128)}, /*index=5*/f32[3,512,512]{2,1,0:T(8,128)}, s32[]{:T(128)}, s32[]{:T(128)}) while((s32[]{:T(128)}, f32[512,128]{1,0:T(8,128)S(1)}, f32[3,512,128]{2,1,0:T(8,128)}, ...), condition=%wide.region_5.6_spmd.clone, body=%wide.region_4.5_spmd.clone.sunk | while | flops 805437440 | bytes 3671647 | solution.py:222
  603.2 17.1 %while.67 = (s32[]{:T(128)}, f32[512,128]{1,0:T(8,128)S(1)}, f32[3,512,128]{2,1,0:T(8,128)}, f32[3,512,512]{2,1,0:T(8,128)}, f32[3,512,128]{2,1,0:T(8,128)}, /*i...) while((s32[]{:T(128)}, f32[512,128]{1,0:T(8,128)S(1)}, f32[3,512,128]{2,1,0:T(8,128)}, ...), condition=%wide.region_7.8_spmd, body=%wide.region_6.7_spmd.sunk | while | flops 805371904 | bytes 3672161 | solution.py:123
  (126 shorter events, 139.3 us)
Async XLA Ops:
  6.5 67.0 %all-gather.12.cloned.1.call-start = ((), (), s32[]{:S(2)}) async-start(), calls=%async_computation | async-start | bytes 3932160 | tf_op jit(solution)/shard_map/all_gather | solution.py:156
  8.6 255.4 %all-gather.16.cloned.1.call-start = ((), (), s32[]{:S(2)}) async-start(), calls=%async_computation.2 | async-start | bytes 1310720 | tf_op jit(solution)/shard_map/all_gather | solution.py:185
  14.1 2.7 copy-start.4
  14.2 3.6 slice-start
  193.2 3.0 copy-start.5
  218.5 15.7 %copy-start.9 = (f32[4,512,128]{2,1,0:T(8,128)S(1)}, f32[4,512,128]{2,1,0:T(8,128)}, u32[]{:S(2)}) copy-start(f32[4,512,128]{2,1,0:T(8,128)} %param.21) | copy-start | bytes 3145732
  221.9 12.4 %collective-permute-start = (f32[512,384]{1,0:T(8,128)S(1)}, f32[512,384]{1,0:T(8,128)S(1)}, u32[]{:S(2)}, u32[]{:S(2)}) collective-permute-start(f32[512,384]{1,0:T(8,128)S(1)} %fusion.61), channel_id=1, source_target_pairs={{4,0},{8,4},{12,8},{16,12},{20,16},{24,20},{28,24},{5,1},{9,5},{13... | collective-permute-start | bytes 2359304 | tf_op jit(solution)/shard_map/ppermute | solution.py:12
  236.1 80.0 %copy-start.12 = (f32[512,128]{1,0:T(8,128)}, f32[512,128]{1,0:T(8,128)S(1)}, u32[]{:S(2)}) copy-start(f32[512,128]{1,0:T(8,128)S(1)} %get-tuple-element.487) | copy-start | bytes 786436
  236.1 62.6 %all-gather.18.cloned.1.call-start = ((), (), s32[]{:S(2)}) async-start(), calls=%async_computation.3 | async-start | bytes 1310720 | tf_op jit(solution)/shard_map/all_gather | solution.py:187
  236.9 86.7 %all-gather.14.cloned.1.call-start = ((), (), s32[]{:S(2)}) async-start(), calls=%async_computation.1 | async-start | bytes 1310720 | tf_op jit(solution)/shard_map/all_gather | solution.py:186
  237.5 117.6 %all-gather.22.cloned.1.call-start = ((), (), s32[]{:S(2)}) async-start(), calls=%async_computation.5 | async-start | bytes 1310720 | tf_op jit(solution)/shard_map/all_gather | solution.py:185
  264.1 1.2 copy-start.2
  294.0 19.1 %collective-permute-start.2 = (f32[512,384]{1,0:T(8,128)}, f32[512,384]{1,0:T(8,128)}, u32[]{:S(2)}, u32[]{:S(2)}) collective-permute-start(f32[512,384]{1,0:T(8,128)} %fusion.56), channel_id=1, source_target_pairs={{4,0},{8,4},{12,8},{16,12},{20,16},{24,20},{28,24},{5,1},{9,5},{13... | collective-permute-start | bytes 2359304 | tf_op jit(solution)/shard_map/ppermute | solution.py:12
  296.8 26.7 %collective-permute-start.1 = (f32[512,384]{1,0:T(8,128)}, f32[512,384]{1,0:T(8,128)}, u32[]{:S(2)}, u32[]{:S(2)}) collective-permute-start(f32[512,384]{1,0:T(8,128)} %fusion.56), channel_id=1, source_target_pairs={{0,4},{4,8},{8,12},{12,16},{16,20},{20,24},{24,28},{1,5},{5,9},{9,... | collective-permute-start | bytes 2359304 | tf_op jit(solution)/shard_map/ppermute | solution.py:12
  326.7 64.8 %all-gather.24.cloned.1.call-start = ((), (), s32[]{:S(2)}) async-start(), calls=%async_computation.6 | async-start | bytes 1310720 | tf_op jit(solution)/shard_map/all_gather | solution.py:187
  329.7 84.9 %all-gather.20.cloned.1.call-start = ((), (), s32[]{:S(2)}) async-start(), calls=%async_computation.4 | async-start | bytes 1310720 | tf_op jit(solution)/shard_map/all_gather | solution.py:186
  332.7 48.3 %copy-start.10 = (f32[512,128]{1,0:T(8,128)S(1)}, f32[512,128]{1,0:T(8,128)}, u32[]{:S(2)}) copy-start(f32[512,128]{1,0:T(8,128)} %convolution_negate_fusion.2) | copy-start | bytes 786436
  332.8 121.4 %all-gather.28.cloned.1.call-start = ((), (), s32[]{:S(2)}) async-start(), calls=%async_computation.8 | async-start | bytes 1310720 | tf_op jit(solution)/shard_map/all_gather | solution.py:185
  355.1 1.2 copy-start
  384.8 21.6 %collective-permute-start.4 = (f32[512,384]{1,0:T(8,128)}, f32[512,384]{1,0:T(8,128)}, u32[]{:S(2)}, u32[]{:S(2)}) collective-permute-start(f32[512,384]{1,0:T(8,128)} %fusion.54), channel_id=1, source_target_pairs={{8,0},{12,4},{16,8},{20,12},{24,16},{28,20},{9,1},{13,5},{17,9},{2... | collective-permute-start | bytes 2359304 | tf_op jit(solution)/shard_map/ppermute | solution.py:12
  388.1 34.7 %collective-permute-start.3 = (f32[512,384]{1,0:T(8,128)}, f32[512,384]{1,0:T(8,128)}, u32[]{:S(2)}, u32[]{:S(2)}) collective-permute-start(f32[512,384]{1,0:T(8,128)} %fusion.54), channel_id=1, source_target_pairs={{0,8},{4,12},{8,16},{12,20},{16,24},{20,28},{1,9},{5,13},{9,17},{1... | collective-permute-start | bytes 2359304 | tf_op jit(solution)/shard_map/ppermute | solution.py:12
  425.9 63.6 %all-gather.30.cloned.1.call-start = ((), (), s32[]{:S(2)}) async-start(), calls=%async_computation.9 | async-start | bytes 1310720 | tf_op jit(solution)/shard_map/all_gather | solution.py:187
  428.9 84.6 %all-gather.26.cloned.1.call-start = ((), (), s32[]{:S(2)}) async-start(), calls=%async_computation.7 | async-start | bytes 1310720 | tf_op jit(solution)/shard_map/all_gather | solution.py:186
  432.1 48.0 %copy-start.11 = (f32[512,128]{1,0:T(8,128)S(1)}, f32[512,128]{1,0:T(8,128)}, u32[]{:S(2)}) copy-start(f32[512,128]{1,0:T(8,128)} %convolution_negate_fusion) | copy-start | bytes 786436
  432.1 112.8 %all-gather.32.cloned.1.call-start = ((), (), s32[]{:S(2)}) async-start(), calls=%async_computation.10 | async-start | bytes 1310720 | tf_op jit(solution)/shard_map/all_gather | solution.py:209
  454.1 1.2 copy-start.1
  483.8 19.0 %collective-permute-start.6 = (f32[512,384]{1,0:T(8,128)}, f32[512,384]{1,0:T(8,128)}, u32[]{:S(2)}, u32[]{:S(2)}) collective-permute-start(f32[512,384]{1,0:T(8,128)} %fusion.52), channel_id=1, source_target_pairs={{16,0},{20,4},{24,8},{28,12},{17,1},{21,5},{25,9},{29,13},{18,2},{... | collective-permute-start | bytes 2359304 | tf_op jit(solution)/shard_map/ppermute | solution.py:12
  488.0 25.5 %collective-permute-start.5 = (f32[512,384]{1,0:T(8,128)}, f32[512,384]{1,0:T(8,128)}, u32[]{:S(2)}, u32[]{:S(2)}) collective-permute-start(f32[512,384]{1,0:T(8,128)} %fusion.52), channel_id=1, source_target_pairs={{0,16},{4,20},{8,24},{12,28},{1,17},{5,21},{9,25},{13,29},{2,18},{... | collective-permute-start | bytes 2359304 | tf_op jit(solution)/shard_map/ppermute | solution.py:12
  545.0 1.2 copy-start.3
  546.2 29.0 %copy-start.6 = (f32[3,512,512]{2,1,0:T(8,128)S(1)}, f32[3,512,512]{2,1,0:T(8,128)}, u32[]{:S(2)}) copy-start(f32[3,512,512]{2,1,0:T(8,128)} %get-tuple-element.786) | copy-start | bytes 9437188
  572.9 9.7 %copy-start.13 = (f32[512,128]{1,0:T(8,128)}, f32[512,128]{1,0:T(8,128)S(1)}, u32[]{:S(2)}) copy-start(f32[512,128]{1,0:T(8,128)S(1)} %fusion.50) | copy-start | bytes 786436
  572.9 8.6 %collective-permute-start.7 = (f32[512,128]{1,0:T(8,128)S(1)}, f32[512,128]{1,0:T(8,128)S(1)}, u32[]{:S(2)}, u32[]{:S(2)}) collective-permute-start(f32[512,128]{1,0:T(8,128)S(1)} %fusion.50), channel_id=1, source_target_pairs={{0,4},{4,8},{8,12},{12,16},{16,20},{20,24},{24,28},{1,5},{5,9},{9,... | collective-permute-start | bytes 786440 | tf_op jit(solution)/shard_map/ppermute | solution.py:12
  575.4 6.1 copy-start.7
  585.6 1.1 copy-start.8
Sparse Core Ops, SparseCore 0:
  8.9 64.5 all-gather.11
  236.3 27.7 all-gather.15
  265.7 28.2 all-gather.17
  295.3 28.1 all-gather.13
  326.8 28.2 all-gather.21
  356.5 28.2 all-gather.23
  386.3 28.2 all-gather.19
  426.0 28.0 all-gather.27
  455.7 28.2 all-gather.29
  485.4 28.0 all-gather.25
  516.7 28.2 all-gather.31

commit v2 on v1

--- a/solution.py
+++ b/solution.py
@@ -113,63 +113,54 @@
     return invert_batch(matrix[None])[0]
 
 
-def backward_sweep(inverses, next_links, advanced):
-
-    def backward(later_block, inputs):
-        inverse, advanced_block, coupling = inputs
-        solved = matmul(inverse, advanced_block - matmul(coupling.T, later_block))
-        return (solved, solved)
-
-    last_state, solved = lax.scan(
-        backward, jnp.zeros_like(advanced[0]), (inverses, advanced, next_links), reverse=True
-    )
-    return solved
-
-
 def on_device(diagonal, lower, right_side):
     blocks = lower.shape[0]
     block_size = lower.shape[1]
     col_share = diagonal.shape[2]
-    rhs_cols = right_side.shape[2]
     interior = blocks - 1
     offset = lax.axis_index("col") * col_share
     has_left = (lax.axis_index("seg") > 0).astype(jnp.float32)
     left_block = lower[0] * has_left
     sep_block = lower[blocks - 1]
-    identity = jnp.eye(block_size, dtype=jnp.float32)
-    left_mask = (jnp.arange(interior) > 0).astype(jnp.float32)[:, None, None]
-    couple = lower[:interior] * left_mask
-    next_links = jnp.concatenate(
-        [couple[1:], jnp.zeros((1, block_size, block_size), jnp.float32)], axis=0
-    )
+    assert interior == 3
+    first_link, second_link = lower[1], lower[2]
     left_cols = lax.dynamic_slice_in_dim(left_block, offset, col_share, 1)
     right_cols = lax.dynamic_slice_in_dim(sep_block, offset, col_share, 0).T
-    empty_cols = jnp.zeros((interior, block_size, col_share), jnp.float32)
-    stacked = jnp.concatenate(
+    outer = jnp.concatenate([diagonal[0], diagonal[2]], axis=0)
+    outer_full = lax.all_gather(outer, "col", axis=1, tiled=True)
+    middle_full = lax.all_gather(diagonal[1], "col", axis=1, tiled=True)
+    outer_inverses = invert_batch(outer_full.reshape(2, block_size, block_size))
+    first_inverse, last_inverse = outer_inverses[0], outer_inverses[1]
+    first_weight = matmul(first_link, first_inverse)
+    last_weight = matmul(second_link.T, last_inverse)
+    schur = (
+        middle_full - matmul(first_weight, first_link.T) - matmul(last_weight, second_link)
+    )
+    middle_inverse = invert_spd(schur)
+    first_rhs = jnp.concatenate([left_cols, right_side[0]], axis=1)
+    last_rhs = jnp.concatenate([right_cols, right_side[2]], axis=1)
+    first_push = matmul(first_weight, first_rhs)
+    last_push = matmul(last_weight, last_rhs)
+    middle_rhs = jnp.concatenate(
         [
-            empty_cols.at[0].set(left_cols),
-            empty_cols.at[interior - 1].set(right_cols),
-            right_side[:interior],
+            -first_push[:, :col_share],
+            -last_push[:, :col_share],
+            right_side[1] - first_push[:, col_share:] - last_push[:, col_share:],
         ],
-        axis=2,
-    )
-    diag_items = lax.all_gather(diagonal[:interior], "col", axis=2, tiled=True)
-
-    def forward(state, inputs):
-        inverse, previous = state
-        diag_block, coupling, rhs_block = inputs
-        schur = diag_block - matmul(coupling, matmul(inverse, coupling.T))
-        new_inverse = invert_spd(schur)
-        advanced = rhs_block - matmul(coupling, matmul(inverse, previous))
-        return ((new_inverse, advanced), (new_inverse, advanced))
-
-    start_state = (identity, jnp.zeros((block_size, stacked.shape[2]), jnp.float32))
-    final_state, (inverses, advanced) = lax.scan(
-        forward, start_state, (diag_items, couple, stacked)
-    )
-    solved = backward_sweep(inverses, next_links, advanced)
-    own_terms = matmul(sep_block, solved[interior - 1])
-    next_terms = passed_along(matmul(left_block.T, solved[0]), "seg", -1)
+        axis=1,
+    )
+    middle_solved = matmul(middle_inverse, middle_rhs)
+    no_cols = jnp.zeros((block_size, col_share), jnp.float32)
+    first_own = matmul(first_inverse, first_rhs)
+    last_own = matmul(last_inverse, last_rhs)
+    first_solved = jnp.concatenate(
+        [first_own[:, :col_share], no_cols, first_own[:, col_share:]], axis=1
+    ) - matmul(first_weight.T, middle_solved)
+    last_solved = jnp.concatenate([no_cols, last_own], axis=1) - matmul(
+        last_weight.T, middle_solved
+    )
+    own_terms = matmul(sep_block, last_solved)
+    next_terms = passed_along(matmul(left_block.T, first_solved), "seg", -1)
     pivot_block = (
         diagonal[blocks - 1] - own_terms[:, col_share : 2 * col_share] - next_terms[:, :col_share]
     )
@@ -209,24 +200,23 @@
     pivot_full = lax.all_gather(pivot_block, "col", axis=1, tiled=True)
     separator = matmul(invert_spd(pivot_full), reduced_rhs)
     left_sep = passed_along(separator, "seg", 1)
-    correction = jnp.zeros((interior, block_size, rhs_cols), jnp.float32)
-    correction = correction.at[0].add(matmul(left_block, left_sep))
-    correction = correction.at[interior - 1].add(matmul(sep_block.T, separator))
-    previous_inverses = jnp.concatenate([identity[None], inverses[:-1]], axis=0)
-
-    def forward_only(previous, inputs):
-        inverse, coupling, rhs_block = inputs
-        advanced_block = rhs_block - matmul(coupling, matmul(inverse, previous))
-        return (advanced_block, advanced_block)
-
-    last_pushed, pushed = lax.scan(
-        forward_only,
-        jnp.zeros((block_size, rhs_cols), jnp.float32),
-        (previous_inverses, couple, correction),
-    )
-    adjust = backward_sweep(inverses, next_links, pushed)
-    interior_part = solved[:, :, 2 * col_share :] - adjust
-    return jnp.concatenate([interior_part, separator[None]], axis=0)
+    first_fix = matmul(left_block, left_sep)
+    last_fix = matmul(sep_block.T, separator)
+    middle_fix = matmul(
+        middle_inverse, matmul(first_weight, first_fix) + matmul(last_weight, last_fix)
+    )
+    return jnp.stack(
+        [
+            first_solved[:, 2 * col_share :]
+            - matmul(first_inverse, first_fix)
+            - matmul(first_weight.T, middle_fix),
+            middle_solved[:, 2 * col_share :] + middle_fix,
+            last_solved[:, 2 * col_share :]
+            - matmul(last_inverse, last_fix)
+            - matmul(last_weight.T, middle_fix),
+            separator,
+        ]
+    )
 
 
 def solution(mesh):

time: 643 us -> 548 us (0.85)
  matrix products: 163 us -> 107 us
  waiting for transfers between devices: 221 us -> 207 us
  other arithmetic: 14.2 us -> 4.91 us
  Pallas kernels: 173 us -> 165 us
    dot_general x54 -> x42, matrix products: 163 us -> 107 us  [matmul(): jnp.dot(left_hand, right_hand, precision=lax.Precision.HIGHEST, preferred...]
    all_gather x1 -> x2, waiting for transfers between devices: 54.2 us -> 42.3 us  [the longest x1 42.3 us: on_device(): outer_full = lax.all_gather(outer, 'col', axis=1, tiled=True)]
    pallas_call x7 -> x6, Pallas kernels: 173 us -> 165 us  [invert_batch(): pl.pallas_call(invert_kernel, out_shape=jax.ShapeDtypeStruct(matrices.sha...]
  transfers between devices with their start and end apart: 19 -> 20, of which waited for: 14 -> 14; matrix products, arithmetic and copies ran while one was open for 10% -> 13% of each run, Pallas kernels for 12% -> 21%
where the time goes in v2:
time: 548 us; the launch traced here: 540 us
  waiting for transfers between devices  207 us (38%)
  Pallas kernels  165 us (30%)
  matrix products  107 us (20%)
  starting transfers between devices  23.4 us (4%)
  local copies, waits for them, and re-layouts  16.8 us (3%)
  between operations  14.7 us (3%)
    pallas_call x6, Pallas kernels, invert_batch(): pl.pallas_call(invert_kernel, out_shape=jax.ShapeDtypeStruct(matrices.sha...  165 us
    dot_general x42, matrix products, matmul(): jnp.dot(left_hand, right_hand, precision=lax.Precision.HIGHEST, preferred...  107 us
    all_gather x3, waiting for transfers between devices, on_device(): lax.all_gather(pivot_block, 'col', axis=1, tiled=True)  60 us
    ppermute x8, waiting for transfers between devices, passed_along(): return lax.ppermute(shard, axis, pairs)  59.5 us
    all_gather x1, waiting for transfers between devices, on_device(): outer_full = lax.all_gather(outer, 'col', axis=1, tiled=True)  42.3 us
    all_gather x1, waiting for transfers between devices, on_device(): pivot_full = lax.all_gather(pivot_block, 'col', axis=1, tiled=True)  22.9 us
    ppermute x8, starting transfers between devices, passed_along(): return lax.ppermute(shard, axis, pairs)  22.3 us
    all_gather x3, waiting for transfers between devices, on_device(): lax.all_gather(sub_block, 'col', axis=1, tiled=True)  20.6 us
  transfers between devices with their start and end apart: 20, of which 14 were waited for; matrix products, arithmetic and copies ran while one was open for 13% of the time, Pallas kernels for 21%

profile of v2, /device:TPU:4, one launch (start us, length us, event | category | flops | bytes accessed | tf_op | source)
XLA Modules:
  0.0 539.6 jit_solution(10707379600221339707)
XLA Ops:
  14.5 42.3 %all-gather.14.cloned.1.call-done = f32[1024,512]{1,0:T(8,128)} async-done(((f32[1024,128]{1,0:T(8,128)}), f32[1024,512]{1,0:T(8,128)}) %all-gather.14.cloned.1.call-update) | async-done | bytes 2097168 | tf_op jit(solution)/shard_map/all_gather | solution.py:130
  58.4 41.5 %invert_spd.6 = f32[2,512,512]{2,1,0:T(8,128)S(1)} custom-call(f32[2,512,512]{2,1,0:T(8,128)S(1)} %bitcast.124), custom_call_target="tpu_custom_call" | custom-call | flops 536870912 | bytes 4194304 | tf_op jit(solution)/shard_map/invert_spd/pallas_call | solution.py:99
  101.9 3.5 fusion.32
  106.3 2.9 fusion.61
  111.1 5.7 %convolution_subtract_fusion.1 = f32[512,512]{1,0:T(8,128)S(1)} fusion(f32[512,512]{1,0:T(8,128)} %copy-done.8, f32[1,512,512]{2,1,0:T(8,128)} %all-gather.36.cloned.1.call-done, f32[4,512,512]{2,1,0:T(8,128)} %param.4), kind=kOutput, calls=%fused_computation.2 | convolution fusion | flops 1610874880 | bytes 4194304 | tf_op jit(solution)/shard_map/dot_general | solution.py:16
  119.2 24.7 %invert_spd.7 = f32[1,512,512]{2,1,0:T(8,128)S(1)} custom-call(f32[1,512,512]{2,1,0:T(8,128)S(1)} %fusion.matrix_ref), custom_call_target="tpu_custom_call" | custom-call | flops 268435456 | bytes 2097152 | tf_op jit(solution)/shard_map/invert_spd/pallas_call | solution.py:99
  144.0 2.4 fusion.60
  150.0 3.4 fusion.22
  153.4 3.0 collective-permute-start
  160.9 4.8 collective-permute-done
  169.0 26.7 %all-gather.18.cloned.1.call-done = f32[512,512]{1,0:T(8,128)} async-done(((f32[512,128]{1,0:T(8,128)}), f32[512,512]{1,0:T(8,128)}) %all-gather.18.cloned.1.call-update) | async-done | bytes 1048592 | tf_op jit(solution)/shard_map/all_gather | solution.py:176
  196.9 24.7 %invert_spd.8 = f32[1,512,512]{2,1,0:T(8,128)S(1)} custom-call(f32[1,512,512]{2,1,0:T(8,128)S(1)} %bitcast.127), custom_call_target="tpu_custom_call" | custom-call | flops 268435456 | bytes 2097152 | tf_op jit(solution)/shard_map/invert_spd/pallas_call | solution.py:99
  221.7 3.7 fusion.15
  225.4 2.8 collective-permute-start.2
  230.2 14.3 %collective-permute-done.2 = f32[512,384]{1,0:T(8,128)} collective-permute-done((f32[512,384]{1,0:T(8,128)}, f32[512,384]{1,0:T(8,128)}, u32[]{:S(2)}, u32[]{:S(2)}) %collective-permute-start.2) | collective-permute-done | bytes 786464 | tf_op jit(solution)/shard_map/ppermute | solution.py:12
  244.5 3.0 fusion.81
  247.5 7.6 %all-gather.16.cloned.1.call-done = f32[512,512]{1,0:T(8,128)} async-done(((f32[512,128]{1,0:T(8,128)}), f32[512,512]{1,0:T(8,128)}) %all-gather.16.cloned.1.call-update) | async-done | bytes 1048592 | tf_op jit(solution)/shard_map/all_gather | solution.py:177
  255.1 3.1 fusion.8
  258.3 3.0 convolution_negate_fusion.2
  261.3 3.0 convolution_negate_fusion.3
  267.0 3.0 fusion.7
  270.0 16.5 %all-gather.24.cloned.1.call-done = f32[512,512]{1,0:T(8,128)} async-done(((f32[512,128]{1,0:T(8,128)}), f32[512,512]{1,0:T(8,128)}) %all-gather.24.cloned.1.call-update) | async-done | bytes 1048592 | tf_op jit(solution)/shard_map/all_gather | solution.py:176
  287.8 24.7 %invert_spd.9 = f32[1,512,512]{2,1,0:T(8,128)S(1)} custom-call(f32[1,512,512]{2,1,0:T(8,128)S(1)} %bitcast.125), custom_call_target="tpu_custom_call" | custom-call | flops 268435456 | bytes 2097152 | tf_op jit(solution)/shard_map/invert_spd/pallas_call | solution.py:99
  312.6 3.8 fusion.13
  316.3 3.4 collective-permute-start.4
  319.7 3.3 collective-permute-start.3
  323.1 14.9 %collective-permute-done.4 = f32[512,384]{1,0:T(8,128)} collective-permute-done((f32[512,384]{1,0:T(8,128)}, f32[512,384]{1,0:T(8,128)}, u32[]{:S(2)}, u32[]{:S(2)}) %collective-permute-start.4) | collective-permute-done | bytes 786464 | tf_op jit(solution)/shard_map/ppermute | solution.py:12
  337.9 3.0 fusion.73
  340.9 5.2 all-gather.22.cloned.1.call-done
  346.1 8.3 %collective-permute-done.3 = f32[512,384]{1,0:T(8,128)} collective-permute-done((f32[512,384]{1,0:T(8,128)}, f32[512,384]{1,0:T(8,128)}, u32[]{:S(2)}, u32[]{:S(2)}) %collective-permute-start.3) | collective-permute-done | bytes 786464 | tf_op jit(solution)/shard_map/ppermute | solution.py:12
  354.4 3.1 fusion.6
  357.6 3.0 convolution_negate_fusion
  360.8 3.0 convolution_negate_fusion.1
  366.1 3.0 fusion.5
  369.1 16.7 %all-gather.30.cloned.1.call-done = f32[512,512]{1,0:T(8,128)} async-done(((f32[512,128]{1,0:T(8,128)}), f32[512,512]{1,0:T(8,128)}) %all-gather.30.cloned.1.call-update) | async-done | bytes 1048592 | tf_op jit(solution)/shard_map/all_gather | solution.py:176
  387.0 24.7 %invert_spd.10 = f32[1,512,512]{2,1,0:T(8,128)S(1)} custom-call(f32[1,512,512]{2,1,0:T(8,128)S(1)} %bitcast.126), custom_call_target="tpu_custom_call" | custom-call | flops 268435456 | bytes 2097152 | tf_op jit(solution)/shard_map/invert_spd/pallas_call | solution.py:99
  411.7 3.8 fusion.11
  415.5 4.1 collective-permute-start.6
  421.2 13.3 %collective-permute-done.6 = f32[512,384]{1,0:T(8,128)} collective-permute-done((f32[512,384]{1,0:T(8,128)}, f32[512,384]{1,0:T(8,128)}, u32[]{:S(2)}, u32[]{:S(2)}) %collective-permute-start.6) | collective-permute-done | bytes 786464 | tf_op jit(solution)/shard_map/ppermute | solution.py:12
  434.5 3.0 fusion.65
  437.5 7.8 %all-gather.28.cloned.1.call-done = f32[512,512]{1,0:T(8,128)} async-done(((f32[512,128]{1,0:T(8,128)}), f32[512,512]{1,0:T(8,128)}) %all-gather.28.cloned.1.call-update) | async-done | bytes 1048592 | tf_op jit(solution)/shard_map/all_gather | solution.py:177
  445.3 3.1 fusion.4
  453.9 22.9 %all-gather.34.cloned.1.call-done = f32[512,512]{1,0:T(8,128)} async-done(((f32[512,128]{1,0:T(8,128)}), f32[512,512]{1,0:T(8,128)}) %all-gather.34.cloned.1.call-update) | async-done | bytes 1048592 | tf_op jit(solution)/shard_map/all_gather | solution.py:200
  478.0 24.7 %invert_spd.11 = f32[1,512,512]{2,1,0:T(8,128)S(1)} custom-call(f32[1,512,512]{2,1,0:T(8,128)S(1)} %bitcast.128), custom_call_target="tpu_custom_call" | custom-call | flops 268435456 | bytes 2097152 | tf_op jit(solution)/shard_map/invert_spd/pallas_call | solution.py:99
  510.6 2.9 convolution_subtract_fusion.5
  513.5 3.8 collective-permute-done.7
  519.4 2.9 convolution_subtract_fusion.7
  527.2 2.4 fusion.1
  (141 shorter events, 64.4 us)
Async XLA Ops:
  6.5 50.3 %all-gather.14.cloned.1.call-start = ((), (), s32[]{:S(2)}) async-start(), calls=%async_computation | async-start | bytes 2621440 | tf_op jit(solution)/shard_map/all_gather | solution.py:130
  9.2 101.8 %all-gather.36.cloned.1.call-start = ((), (), s32[]{:S(2)}) async-start(), calls=%async_computation.11 | async-start | bytes 1310720 | tf_op jit(solution)/shard_map/all_gather | solution.py:131
  10.0 185.7 %all-gather.18.cloned.1.call-start = ((), (), s32[]{:S(2)}) async-start(), calls=%async_computation.2 | async-start | bytes 1310720 | tf_op jit(solution)/shard_map/all_gather | solution.py:176
  10.0 1.9 copy-start.30
  12.0 44.9 %copy-start.14 = (f32[1,512,512]{2,1,0:T(8,128)}, f32[1,512,512]{2,1,0:T(8,128)S(1)}, u32[]{:S(2)}) copy-start(f32[1,512,512]{2,1,0:T(8,128)S(1)} %get-tuple-element.5) | copy-start | bytes 3145732
  12.8 87.1 %copy-start.25 = (f32[512,128]{1,0:T(8,128)}, f32[512,128]{1,0:T(8,128)S(1)}, u32[]{:S(2)}) copy-start(f32[512,128]{1,0:T(8,128)S(1)} %get-tuple-element.11) | copy-start | bytes 786436
  58.4 43.4 %copy-start.12 = (f32[4,512,512]{2,1,0:T(8,128)S(1)}, f32[4,512,512]{2,1,0:T(8,128)}, u32[]{:S(2)}) copy-start(f32[4,512,512]{2,1,0:T(8,128)} %param.4) | copy-start | bytes 12582916
  111.0 5.8 %copy-start.5 = (f32[512,512]{1,0:T(8,128)}, f32[512,512]{1,0:T(8,128)S(1)}, u32[]{:S(2)}) copy-start(f32[512,512]{1,0:T(8,128)S(1)} %fusion.29) | copy-start | bytes 3145732
  111.1 5.8 %copy-start.13 = (f32[4,512,512]{2,1,0:T(8,128)S(1)}, f32[4,512,512]{2,1,0:T(8,128)}, u32[]{:S(2)}) copy-start(f32[4,512,512]{2,1,0:T(8,128)} %param.4) | copy-start | bytes 12582916
  116.8 27.1 %copy-start.26 = (f32[512,256]{0,1:T(8,128)S(1)}, f32[512,256]{0,1:T(8,128)}, u32[]{:S(2)}) copy-start(f32[512,256]{0,1:T(8,128)} %fusion.38) | copy-start | bytes 1572868
  116.8 27.2 %copy-start.23 = (f32[1,128,512]{1,2,0:T(8,128)S(1)}, f32[1,128,512]{1,2,0:T(8,128)}, u32[]{:S(2)}) copy-start(f32[1,128,512]{1,2,0:T(8,128)} %copy.4) | copy-start | bytes 786436
  116.9 27.2 %copy-start.24 = (f32[512,128]{1,0:T(8,128)S(1)}, f32[512,128]{1,0:T(8,128)}, u32[]{:S(2)}) copy-start(f32[512,128]{1,0:T(8,128)} %get-tuple-element.10) | copy-start | bytes 786436
  116.9 29.6 %copy-start.27 = (f32[512,256]{0,1:T(8,128)S(1)}, f32[512,256]{0,1:T(8,128)}, u32[]{:S(2)}) copy-start(f32[512,256]{0,1:T(8,128)} %fusion.61) | copy-start | bytes 1572868
  116.9 29.6 %copy-start.32 = (f32[1,512,128]{1,2,0:T(8,128)S(1)}, f32[1,512,128]{1,2,0:T(8,128)}, u32[]{:S(2)}) copy-start(f32[1,512,128]{1,2,0:T(8,128)} %copy.42) | copy-start | bytes 786436
  144.0 4.5 copy-start.9
  146.5 3.5 copy-start.15
  148.5 10.6 %copy-start.16 = (f32[512,384]{1,0:T(8,128)}, f32[512,384]{1,0:T(8,128)S(1)}, u32[]{:S(2)}) copy-start(f32[512,384]{1,0:T(8,128)S(1)} %fusion.26) | copy-start | bytes 2359300
  148.5 9.1 %copy-start.6 = (f32[512,512]{1,0:T(8,128)S(1)}, f32[512,512]{1,0:T(8,128)}, u32[]{:S(2)}) copy-start(f32[512,512]{1,0:T(8,128)} %copy-done.5) | copy-start | bytes 3145732
  150.0 10.9 %copy-start.17 = (f32[512,384]{0,1:T(8,128)}, f32[512,384]{0,1:T(8,128)S(1)}, u32[]{:S(2)}) copy-start(f32[512,384]{0,1:T(8,128)S(1)} %convolution_subtract_fusion.3) | copy-start | bytes 2359300
  153.4 12.4 %collective-permute-start = (f32[512,384]{1,0:T(8,128)S(1)}, f32[512,384]{1,0:T(8,128)S(1)}, u32[]{:S(2)}, u32[]{:S(2)}) collective-permute-start(f32[512,384]{1,0:T(8,128)S(1)} %fusion.22), channel_id=1, source_target_pairs={{4,0},{8,4},{12,8},{16,12},{20,16},{24,20},{28,24},{5,1},{9,5},{13... | collective-permute-start | bytes 2359304 | tf_op jit(solution)/shard_map/ppermute | solution.py:12
  159.1 6.7 %copy-start.18 = (f32[512,384]{0,1:T(8,128)}, f32[512,384]{0,1:T(8,128)S(1)}, u32[]{:S(2)}) copy-start(f32[512,384]{0,1:T(8,128)S(1)} %convolution_subtract_fusion.2) | copy-start | bytes 2359300
  167.7 90.5 %copy-start.20 = (f32[512,128]{1,0:T(8,128)}, f32[512,128]{1,0:T(8,128)S(1)}, u32[]{:S(2)}) copy-start(f32[512,128]{1,0:T(8,128)S(1)} %get-tuple-element.7) | copy-start | bytes 786436
  167.8 62.4 %all-gather.20.cloned.1.call-start = ((), (), s32[]{:S(2)}) async-start(), calls=%async_computation.3 | async-start | bytes 1310720 | tf_op jit(solution)/shard_map/all_gather | solution.py:178
  168.3 86.7 %all-gather.16.cloned.1.call-start = ((), (), s32[]{:S(2)}) async-start(), calls=%async_computation.1 | async-start | bytes 1310720 | tf_op jit(solution)/shard_map/all_gather | solution.py:177
  168.9 117.7 %all-gather.24.cloned.1.call-start = ((), (), s32[]{:S(2)}) async-start(), calls=%async_computation.5 | async-start | bytes 1310720 | tf_op jit(solution)/shard_map/all_gather | solution.py:176
  225.4 19.1 %collective-permute-start.2 = (f32[512,384]{1,0:T(8,128)}, f32[512,384]{1,0:T(8,128)}, u32[]{:S(2)}, u32[]{:S(2)}) collective-permute-start(f32[512,384]{1,0:T(8,128)} %fusion.15), channel_id=1, source_target_pairs={{4,0},{8,4},{12,8},{16,12},{20,16},{24,20},{28,24},{5,1},{9,5},{13... | collective-permute-start | bytes 2359304 | tf_op jit(solution)/shard_map/ppermute | solution.py:12
  228.2 26.9 %collective-permute-start.1 = (f32[512,384]{1,0:T(8,128)}, f32[512,384]{1,0:T(8,128)}, u32[]{:S(2)}, u32[]{:S(2)}) collective-permute-start(f32[512,384]{1,0:T(8,128)} %fusion.15), channel_id=1, source_target_pairs={{0,4},{4,8},{8,12},{12,16},{16,20},{20,24},{24,28},{1,5},{5,9},{9,... | collective-permute-start | bytes 2359304 | tf_op jit(solution)/shard_map/ppermute | solution.py:12
  258.2 64.8 %all-gather.26.cloned.1.call-start = ((), (), s32[]{:S(2)}) async-start(), calls=%async_computation.6 | async-start | bytes 1310720 | tf_op jit(solution)/shard_map/all_gather | solution.py:178
  261.2 51.3 %copy-start.19 = (f32[512,128]{1,0:T(8,128)S(1)}, f32[512,128]{1,0:T(8,128)}, u32[]{:S(2)}) copy-start(f32[512,128]{1,0:T(8,128)} %convolution_negate_fusion.2) | copy-start | bytes 786436
  261.2 84.8 %all-gather.22.cloned.1.call-start = ((), (), s32[]{:S(2)}) async-start(), calls=%async_computation.4 | async-start | bytes 1310720 | tf_op jit(solution)/shard_map/all_gather | solution.py:177
  264.3 121.5 %all-gather.30.cloned.1.call-start = ((), (), s32[]{:S(2)}) async-start(), calls=%async_computation.8 | async-start | bytes 1310720 | tf_op jit(solution)/shard_map/all_gather | solution.py:176
  316.3 21.6 %collective-permute-start.4 = (f32[512,384]{1,0:T(8,128)}, f32[512,384]{1,0:T(8,128)}, u32[]{:S(2)}, u32[]{:S(2)}) collective-permute-start(f32[512,384]{1,0:T(8,128)} %fusion.13), channel_id=1, source_target_pairs={{8,0},{12,4},{16,8},{20,12},{24,16},{28,20},{9,1},{13,5},{17,9},{2... | collective-permute-start | bytes 2359304 | tf_op jit(solution)/shard_map/ppermute | solution.py:12
  319.7 34.7 %collective-permute-start.3 = (f32[512,384]{1,0:T(8,128)}, f32[512,384]{1,0:T(8,128)}, u32[]{:S(2)}, u32[]{:S(2)}) collective-permute-start(f32[512,384]{1,0:T(8,128)} %fusion.13), channel_id=1, source_target_pairs={{0,8},{4,12},{8,16},{12,20},{16,24},{20,28},{1,9},{5,13},{9,17},{1... | collective-permute-start | bytes 2359304 | tf_op jit(solution)/shard_map/ppermute | solution.py:12
  340.9 25.2 %copy-start.22 = (f32[512,128]{1,0:T(8,128)S(1)}, f32[512,128]{1,0:T(8,128)}, u32[]{:S(2)}) copy-start(f32[512,128]{1,0:T(8,128)} %fusion.7) | copy-start | bytes 786436
  357.6 63.6 %all-gather.32.cloned.1.call-start = ((), (), s32[]{:S(2)}) async-start(), calls=%async_computation.9 | async-start | bytes 1310720 | tf_op jit(solution)/shard_map/all_gather | solution.py:178
  360.6 84.7 %all-gather.28.cloned.1.call-start = ((), (), s32[]{:S(2)}) async-start(), calls=%async_computation.7 | async-start | bytes 1310720 | tf_op jit(solution)/shard_map/all_gather | solution.py:177
  363.8 113.0 %all-gather.34.cloned.1.call-start = ((), (), s32[]{:S(2)}) async-start(), calls=%async_computation.10 | async-start | bytes 1310720 | tf_op jit(solution)/shard_map/all_gather | solution.py:200
  387.0 61.4 %slice-start = ((f32[512,384]{1,0:T(8,128)}), f32[512,128]{1,0:T(8,128)S(1)}, s32[]{:S(2)}) async-start(f32[512,384]{1,0:T(8,128)} %copy-done.16), calls=%async_computation.12 | async-start | bytes 524288 | tf_op jit(solution)/shard_map/slice | solution.py:213
  415.5 19.0 %collective-permute-start.6 = (f32[512,384]{1,0:T(8,128)}, f32[512,384]{1,0:T(8,128)}, u32[]{:S(2)}, u32[]{:S(2)}) collective-permute-start(f32[512,384]{1,0:T(8,128)} %fusion.11), channel_id=1, source_target_pairs={{16,0},{20,4},{24,8},{28,12},{17,1},{21,5},{25,9},{29,13},{18,2},{... | collective-permute-start | bytes 2359304 | tf_op jit(solution)/shard_map/ppermute | solution.py:12
  419.7 25.6 %collective-permute-start.5 = (f32[512,384]{1,0:T(8,128)}, f32[512,384]{1,0:T(8,128)}, u32[]{:S(2)}, u32[]{:S(2)}) collective-permute-start(f32[512,384]{1,0:T(8,128)} %fusion.11), channel_id=1, source_target_pairs={{0,16},{4,20},{8,24},{12,28},{1,17},{5,21},{9,25},{13,29},{2,18},{... | collective-permute-start | bytes 2359304 | tf_op jit(solution)/shard_map/ppermute | solution.py:12
  508.3 14.0 %copy-start.10 = (f32[512,512]{1,0:T(8,128)S(1)}, f32[512,512]{1,0:T(8,128)}, u32[]{:S(2)}) copy-start(f32[512,512]{1,0:T(8,128)} %copy-done.8) | copy-start | bytes 3145732
  508.3 15.9 %copy-start.7 = (f32[512,512]{1,0:T(8,128)S(1)}, f32[512,512]{1,0:T(8,128)}, u32[]{:S(2)}) copy-start(f32[512,512]{1,0:T(8,128)} %copy-done.5) | copy-start | bytes 3145732
  508.3 8.9 %collective-permute-start.7 = (f32[512,128]{1,0:T(8,128)}, f32[512,128]{1,0:T(8,128)S(1)}, u32[]{:S(2)}, u32[]{:S(2)}) collective-permute-start(f32[512,128]{1,0:T(8,128)} %copy-done.21), channel_id=1, source_target_pairs={{0,4},{4,8},{8,12},{12,16},{16,20},{20,24},{24,28},{1,5},{5,9},{9,... | collective-permute-start | bytes 786440 | tf_op jit(solution)/shard_map/ppermute | solution.py:12
  522.3 4.8 copy-start.28
  522.3 7.3 %copy-start.11 = (f32[512,512]{1,0:T(8,128)S(1)}, f32[512,512]{1,0:T(8,128)}, u32[]{:S(2)}) copy-start(f32[512,512]{1,0:T(8,128)} %copy-done.8) | copy-start | bytes 3145732
  522.3 7.3 %copy-start.29 = (f32[512,128]{0,1:T(8,128)S(1)}, f32[512,128]{0,1:T(8,128)}, u32[]{:S(2)}) copy-start(f32[512,128]{0,1:T(8,128)} %convolution_subtract_fusion.7) | copy-start | bytes 786436
  524.2 6.7 %copy-start.31 = (f32[512,128]{0,1:T(8,128)S(1)}, f32[512,128]{0,1:T(8,128)}, u32[]{:S(2)}) copy-start(f32[512,128]{0,1:T(8,128)} %copy.43) | copy-start | bytes 786436
  526.0 4.9 copy-start.33
  (7 other events, 8.2 us)
Sparse Core Ops, SparseCore 0:
  9.4 47.4 all-gather.13
  58.4 27.3 all-gather.35
  167.9 27.7 all-gather.17
  197.1 28.2 all-gather.19
  226.8 28.2 all-gather.15
  258.3 28.2 all-gather.23
  288.2 28.2 all-gather.25
  318.0 28.0 all-gather.21
  357.7 28.0 all-gather.29
  387.2 28.2 all-gather.31
  417.0 28.2 all-gather.27
  448.6 28.2 all-gather.33
